TPU v7x, 32 devices: a whole 2x2x4 slice. The times are simulated.
32 devices in a mesh: scen: 16 (over z, y, x), fac: 2 (over core).
Axes of the slice: x: 2, y: 2, z: 4, core: 2. Of those that a mesh axis runs over, the one named last changes fastest.
Arguments:
- scenarios: bfloat16 [256, 8192], P(('scen', 'fac')), may hold values from -40 to 40
Outputs:
- shrunk: float32 [8192, 8192], P('scen', 'fac')
- shrinkage: float32 [], replicated
- col_mean: float32 [8192], P('fac')
All inputs are finite; a program needn't handle non-finite values.
Results may differ from a plain program's by a relative error of at most 0.0008.
Values may be sent and summed in bfloat16 or wider, within the bound.
A program may use at most 64 MiB of HBM per device.

v0:
```python
import jax
import jax.numpy as jnp
from jax import lax
from jax.sharding import PartitionSpec as P


def on_device(scenarios):
    row_count = scenarios.shape[0]
    factors = scenarios.shape[1]
    scen_size = lax.axis_size("scen")
    fac_size = lax.axis_size("fac")
    total_rows = row_count * scen_size * fac_size
    group_width = factors // scen_size
    block_width = factors // fac_size
    owner_idx = lax.axis_index("scen")
    block_idx = lax.axis_index("fac")
    col_total = lax.psum(jnp.sum(scenarios.astype(jnp.float32), axis=0), ("scen", "fac"))
    col_mean = col_total / total_rows
    centered = (scenarios.astype(jnp.float32) - col_mean).astype(jnp.bfloat16)
    as_float = centered.astype(jnp.float32)
    squared = jnp.sum(as_float * as_float, axis=1)
    trace_part = jnp.sum(squared)
    fourth_part = jnp.sum(squared * squared)
    trace_total, fourth_total = lax.psum((trace_part, fourth_part), ("scen", "fac"))
    contract = (((0,), (0,)), ((), ()))
    local_rows = lax.all_gather(centered, "fac", axis=0, tiled=True)
    narrow_all = lax.all_to_all(local_rows, "scen", split_axis=1, concat_axis=0, tiled=True)
    wide_cols = lax.dynamic_slice_in_dim(local_rows, block_idx * block_width, block_width, 1)
    summed = lax.dot_general(
        narrow_all,
        lax.all_gather(wide_cols, "scen", axis=0, tiled=True),
        contract,
        preferred_element_type=jnp.float32,
    )
    covariance = summed / total_rows
    row_index = owner_idx * group_width + lax.broadcasted_iota(
        jnp.int32, (group_width, block_width), 0
    )
    col_index = block_idx * block_width + lax.broadcasted_iota(
        jnp.int32, (group_width, block_width), 1
    )
    diag_mask = (row_index == col_index).astype(jnp.float32)
    mu_scale = trace_total / (total_rows * factors)
    distance = covariance - mu_scale * diag_mask
    frob_sum = lax.psum(jnp.sum(distance * distance), ("scen", "fac"))
    spread = frob_sum / factors
    norm_sq = factors * (spread + mu_scale * mu_scale)
    beta_value = (fourth_total / total_rows - norm_sq) / (factors * total_rows)
    shrinkage = beta_value / spread
    shrunk = (1.0 - shrinkage) * covariance + shrinkage * mu_scale * diag_mask
    mean_block = lax.dynamic_slice_in_dim(col_mean, block_idx * block_width, block_width, 0)
    return (shrunk, shrinkage, mean_block)


def solution(mesh):
    return jax.shard_map(
        on_device,
        mesh=mesh,
        in_specs=(P(("scen", "fac"), None),),
        out_specs=(P("scen", "fac"), P(), P("fac")),
        check_vma=False,
    )
```

profile of v0, /device:TPU:0, one launch (start us, length us, event | category | flops | bytes accessed | tf_op | source)
XLA Modules:
  0.0 179.8 jit_solution(12894808986534440513)
XLA Ops:
  7.2 0.0 all-gather.2.cloned.1.call-start
  7.2 1.0 convert_reduce_fusion
  8.2 42.1 %psum.28 = f32[8192]{0:T(1024)S(1)} all-reduce(f32[8192]{0:T(1024)S(1)} %convert_reduce_fusion), channel_id=1, replica_groups=mesh['scen'=16,'fac'=2] {'scen','fac'}, use_global_device_ids=true, to_apply=%region_1.0 | all-reduce | flops 8192 | bytes 65536 | tf_op jit(solution)/shard_map/psum | solution.py:17
  50.4 1.6 fusion.5
  52.0 2.0 %all_gather.6 = bf16[16,8192]{1,0:T(8,128)(2,1)S(1)} all-gather(bf16[8,8192]{1,0:T(8,128)(2,1)S(1)} %get-tuple-element.7), channel_id=1, replica_groups=mesh['scen'=16,'fac'=2] {'fac'}, dimensions={0}, use_global_device_ids=true | all-gather | bytes 393216 | tf_op jit(solution)/shard_map/all_gather | solution.py:26
  54.0 0.7 constant_dynamic-slice_fusion
  54.6 0.0 all-gather.2.cloned.1.call-update
  54.6 0.7 copy.8
  55.4 5.4 %all-to-all-start = ((bf16[16,16,512]{2,0,1:T(8,128)(2,1)}), bf16[16,16,512]{2,0,1:T(8,128)(2,1)S(1)}, u32[]{:S(2)}, u32[]{:S(2)}) async-start(bf16[16,16,512]{2,0,1:T(8,128)(2,1)} %bitcast.8), calls=%async_computation | async-start | bytes 524288 | tf_op jit(solution)/shard_map/all_to_all | solution.py:27
  60.8 41.2 %psum.30 = f32[]{:T(128)} all-reduce(f32[]{:T(128)} %get-tuple-element.3), channel_id=1, replica_groups=mesh['scen'=16,'fac'=2] {'scen','fac'}, use_global_device_ids=true, to_apply=%region_6.0 | all-reduce | flops 1 | bytes 8 | tf_op jit(solution)/shard_map/psum | solution.py:24
  102.0 0.6 dynamic_slice.7
  104.6 0.7 multiply_reduce_fusion
  105.2 0.0 all-to-all-done
  105.2 10.7 %all-gather.2.cloned.1.call-done = bf16[256,4096]{1,0:T(8,128)(2,1)} async-done(((bf16[16,4096]{1,0:T(8,128)(2,1)}), bf16[256,4096]{1,0:T(8,128)(2,1)}) %all-gather.2.cloned.1.call-update) | async-done | bytes 2097168 | tf_op jit(solution)/shard_map/all_gather | solution.py:31
  115.9 6.8 %fusion.2 = (f32[]{:T(128)}, f32[512,4096]{1,0:T(8,128)}) fusion(f32[]{:T(128)S(6)} %div.32, s32[4096]{0:T(1024)S(1)} %iota_add_fusion, s32[512]{0:T(512)S(1)} %iota_add_fusion.1, bf16[256,512]{1,0:T(8,128)(2,1)S(1)} %bitcast.10, bf16[256,4096]{1,0:T(8,128)(2,1)} %all-gather.2.cloned.1.call-done), kind=kOutput, calls=%fused_computation.4 | convolution fusion | flops 1086324736 | bytes 10766344 | tf_op jit(solution)/shard_map/dot_general | solution.py:29
  122.8 39.0 %all-reduce = (f32[]{:T(128)}, f32[]{:T(128)}) all-reduce(f32[]{:T(128)} %multiply_reduce_fusion, f32[]{:T(128)} %get-tuple-element.8), channel_id=1, replica_groups=mesh['scen'=16,'fac'=2] {'scen','fac'}, use_global_device_ids=true, to_apply=%region_4.0 | all-reduce | flops 2 | bytes 16 | tf_op jit(solution)/shard_map/psum | solution.py:24
  163.1 8.7 %fusion.3 = f32[512,4096]{1,0:T(8,128)} fusion(f32[512,4096]{1,0:T(8,128)} %get-tuple-element.9, f32[]{:T(128)S(6)} %mul.61, f32[]{:T(128)S(6)} %mul.58, s32[4096]{0:T(1024)S(1)} %iota_add_fusion, s32[512]{0:T(512)S(1)} %iota_add_fusion.1), kind=kLoop, calls=%fused_computation.5 | loop fusion | flops 8388608 | bytes 16795656 | tf_op jit(solution)/shard_map/add | solution.py:50
  (3 shorter events, 0.0 us)
Async XLA Ops:
  7.2 108.7 %all-gather.2.cloned.1.call-start = ((), (), s32[]{:S(2)}) async-start(), calls=%async_computation.1 | async-start | bytes 2228224 | tf_op jit(solution)/shard_map/all_gather | solution.py:31
  55.4 49.9 %all-to-all-start = ((bf16[16,16,512]{2,0,1:T(8,128)(2,1)}), bf16[16,16,512]{2,0,1:T(8,128)(2,1)S(1)}, u32[]{:S(2)}, u32[]{:S(2)}) async-start(bf16[16,16,512]{2,0,1:T(8,128)(2,1)} %bitcast.8), calls=%async_computation | async-start | bytes 524288 | tf_op jit(solution)/shard_map/all_to_all | solution.py:27
Sparse Core Ops, SparseCore 0:
  54.8 61.1 all-gather.1
where the time goes:
time: 181 us; the launch traced here: 180 us
  blocking collectives  124 us (69%)
  between operations  18.5 us (10%)
  other arithmetic  12 us (7%)
  waiting for transfers between devices  10.7 us (6%)
  matrix products  6.84 us (4%)
  starting transfers between devices  5.46 us (3%)
  local copies, waits for them, and re-layouts  2 us (1%)
    psum x2, blocking collectives, on_device(): lax.psum((trace_part, fourth_part), ('scen', 'fac'))  80.2 us
    psum x1, blocking collectives, on_device(): lax.psum(jnp.sum(scenarios.astype(jnp.float32), axis=0), ('scen', 'fac'))  42.1 us
    all_gather x1, waiting for transfers between devices, on_device(): lax.all_gather(wide_cols, 'scen', axis=0, tiled=True)  10.7 us
    add x1, other arithmetic, on_device(): shrunk = (1.0 - shrinkage) * covariance + shrinkage * mu_scale * diag_mask  8.69 us
    dot_general x1, matrix products, on_device(): lax.dot_general(narrow_all, lax.all_gather(wide_cols, 'scen', axis=0, til...  6.84 us
    all_to_all x1, starting transfers between devices, on_device(): lax.all_to_all(local_rows, 'scen', split_axis=1, concat_axis=0, tiled=True)  5.42 us
  transfers between devices with their start and end apart: 2, of which 1 were waited for; matrix products, arithmetic and copies ran while one was open for 1% of the time, Pallas kernels for 0%

commit v1 on v0

--- a/solution.py
+++ b/solution.py
@@ -1,7 +1,301 @@
+import functools
+
 import jax
 import jax.numpy as jnp
 from jax import lax
+from jax.experimental import pallas as pl
+from jax.experimental.pallas import tpu as pltpu
 from jax.sharding import PartitionSpec as P
+
+MESH = pl.DeviceIdType.MESH
+F32 = jnp.float32
+BF16 = jnp.bfloat16
+
+
+def gather_kernel(lines, rows_ref, mine_ref, other_ref, local_sem, pair_sems, z_sems, x_sems, y_sems, d_sems, core_sems):
+    scen = lax.axis_index("scen")
+    fac = lax.axis_index("fac")
+    z, y, x = scen // 4, (scen // 2) % 2, scen % 2
+    half = mine_ref.shape[-1]
+    mid = half // 2
+
+    def chip(k, yy, xx):
+        return k * 4 + yy * 2 + xx
+
+    x_next = (chip(z, y, 1 - x), fac)
+    y_next = (chip(z, 1 - y, x), fac)
+    partner = (scen, 1 - fac)
+    above = (chip(jnp.minimum(z + 1, lines - 1), y, x), fac)
+    below = (chip(jnp.maximum(z - 1, 0), y, x), fac)
+    has_above = z < lines - 1
+    has_below = z > 0
+
+    barrier = pltpu.get_barrier_semaphore()
+    for device in (x_next, y_next, partner):
+        pl.semaphore_signal(barrier, inc=1, device_id=device, device_id_type=MESH)
+
+    @pl.when(has_above)
+    def _():
+        pl.semaphore_signal(barrier, inc=1, device_id=above, device_id_type=MESH)
+
+    @pl.when(has_below)
+    def _():
+        pl.semaphore_signal(barrier, inc=1, device_id=below, device_id_type=MESH)
+
+    pl.semaphore_wait(barrier, 3 + has_above.astype(jnp.int32) + has_below.astype(jnp.int32))
+
+    def copy(src, dst, sems, i, device):
+        return pltpu.make_async_remote_copy(
+            src_ref=src, dst_ref=dst, send_sem=sems.at[0, i], recv_sem=sems.at[1, i], device_id=device, device_id_type=MESH
+        )
+
+    def block(c):
+        return mine_ref.at[c]
+
+    keep = pltpu.make_async_copy(rows_ref.at[:, pl.ds(pl.multiple_of(fac * half, half), half)], mine_ref.at[scen, fac], local_sem.at[0])
+    keep.start()
+    give = copy(
+        rows_ref.at[:, pl.ds(pl.multiple_of((1 - fac) * half, half), half)], mine_ref.at[scen, fac], pair_sems, 0, partner
+    )
+    give.start()
+    keep.wait()
+    give.wait_recv()
+
+    def up(k):
+        return copy(block(chip(k, y, x)), block(chip(k, y, x)), z_sems, k, above)
+
+    def down(k):
+        return pltpu.make_async_remote_copy(
+            src_ref=block(chip(k, y, x)),
+            dst_ref=block(chip(k, y, x)),
+            send_sem=z_sems.at[2, k],
+            recv_sem=z_sems.at[1, k],
+            device_id=below,
+            device_id_type=MESH,
+        )
+
+    def to_x(k):
+        return copy(block(chip(k, y, x)), block(chip(k, y, x)), x_sems, k, x_next)
+
+    def to_y(k):
+        return copy(block(chip(k, y, x)), block(chip(k, y, x)), y_sems, k, y_next)
+
+    def part(c, i):
+        return mine_ref.at[c, :, :, pl.ds(i * mid, mid)]
+
+    def diag_x(k):
+        c = chip(k, 1 - y, x)
+        return copy(part(c, 0), part(c, 0), d_sems, 2 * k, x_next)
+
+    def diag_y(k):
+        c = chip(k, y, 1 - x)
+        return copy(part(c, 1), part(c, 1), d_sems, 2 * k + 1, y_next)
+
+    def to_core(c):
+        return copy(mine_ref.at[c], other_ref.at[c], core_sems, c, partner)
+
+    def line_step(k, ups, downs, arrived):
+        if arrived:
+            up(k).wait_recv()
+        to_x(k).start()
+        to_y(k).start()
+        if ups:
+            @pl.when(has_above)
+            def _():
+                up(k).start()
+        if downs:
+            @pl.when(has_below)
+            def _():
+                down(k).start()
+        to_core(chip(k, y, x)).start()
+
+    def side_step(k):
+        to_x(k).wait_recv()
+        diag_y(k).start()
+        to_core(chip(k, y, 1 - x)).start()
+        to_y(k).wait_recv()
+        diag_x(k).start()
+        to_core(chip(k, 1 - y, x)).start()
+
+    def diag_step(k):
+        diag_x(k).wait_recv()
+        diag_y(k).wait_recv()
+        to_core(chip(k, 1 - y, 1 - x)).start()
+
+    def each(d, step):
+        if d == 0:
+            step(z, 0)
+            return
+
+        @pl.when(z - d >= 0)
+        def _():
+            step(z - d, -1)
+
+        @pl.when(z + d < lines)
+        def _():
+            step(z + d, 1)
+
+    line_step(z, True, True, False)
+    for d in range(1, lines):
+        each(d, lambda k, sign: line_step(k, sign < 0, sign > 0, True))
+        each(d - 1, lambda k, sign: side_step(k))
+    each(lines - 1, lambda k, sign: side_step(k))
+    for d in range(lines):
+        each(d, lambda k, sign: diag_step(k))
+
+    give.wait_send()
+    for k in range(lines):
+        to_x(k).wait_send()
+        to_y(k).wait_send()
+        diag_x(k).wait_send()
+        diag_y(k).wait_send()
+
+        @pl.when((k <= z) & has_above)
+        def _():
+            up(k).wait_send()
+
+        @pl.when((k >= z) & has_below)
+        def _():
+            down(k).wait_send()
+    for c in range(4 * lines):
+        to_core(c).wait()
+
+
+def shrink_kernel(steps, mine_ref, other_ref, out_ref, shrinkage_ref, mean_ref, cols, cols_other, narrow, scalars):
+    step = pl.program_id(0)
+    scen = lax.axis_index("scen")
+    fac = lax.axis_index("fac")
+    blocks, rows, half = mine_ref.shape
+    total_rows = blocks * rows
+    factors = 2 * half
+    width = narrow.shape[0]
+    tall = out_ref.shape[0]
+    per_half = half // width
+    in_mine = scen // per_half == fac
+    offset = (scen % per_half) * width
+
+    @pl.when(step == 0)
+    def _():
+        chunk = 512
+
+        def centre(src, dst, i, mean_out):
+            at = pl.ds(pl.multiple_of(i * chunk, chunk), chunk)
+            total = src[0, :, at].astype(F32)
+            for j in range(1, blocks):
+                total = total + src[j, :, at].astype(F32)
+            mean = jnp.sum(total, axis=0, keepdims=True) / total_rows
+            if mean_out is not None:
+                mean_out[:, at] = mean
+            for j in range(0, blocks, 2):
+                pair = src[pl.ds(j, 2), :, at].astype(F32).reshape(2 * rows, chunk)
+                dst[pl.ds(j * rows, 2 * rows), at] = (pair - mean).astype(BF16)
+
+        @pl.loop(0, half // chunk)
+        def _(i):
+            centre(mine_ref, cols, i, mean_ref)
+            centre(other_ref, cols_other, i, None)
+
+        at = pl.ds(pl.multiple_of(offset, width), width)
+
+        @pl.when(in_mine)
+        def _():
+            narrow[...] = cols[:, at].T
+
+        @pl.when(jnp.logical_not(in_mine))
+        def _():
+            narrow[...] = cols_other[:, at].T
+
+        across = (((1,), (1,)), ((), ()))
+        gram = lax.dot_general(cols[...], cols[...], across, preferred_element_type=F32)
+        gram = gram + lax.dot_general(cols_other[...], cols_other[...], across, preferred_element_type=F32)
+        on_diag = lax.broadcasted_iota(jnp.int32, gram.shape, 0) == lax.broadcasted_iota(jnp.int32, gram.shape, 1)
+        gram_sq = gram * gram
+
+        def total_of(v):
+            return jnp.sum(jnp.sum(v, axis=0, keepdims=True), axis=1, keepdims=True)
+
+        trace_total = total_of(jnp.where(on_diag, gram, 0.0))
+        fourth_total = total_of(jnp.where(on_diag, gram_sq, 0.0))
+        cov_sq = total_of(gram_sq) / (total_rows * total_rows)
+        mu_scale = trace_total / (total_rows * factors)
+        spread = (cov_sq - factors * mu_scale * mu_scale) / factors
+        norm_sq = factors * (spread + mu_scale * mu_scale)
+        beta_value = (fourth_total / total_rows - norm_sq) / (factors * total_rows)
+        shrinkage = beta_value / spread
+        shrinkage_ref[...] = shrinkage
+        scalars[0:1, :] = jnp.broadcast_to((1.0 - shrinkage) / total_rows, (1, 128))
+        scalars[1:2, :] = jnp.broadcast_to(shrinkage * mu_scale, (1, 128))
+
+    scale = scalars[0:1, 0:1]
+    left = narrow[pl.ds(pl.multiple_of(step * tall, tall), tall), :]
+    piece = 1024
+    for i in range(half // piece):
+        at = pl.ds(i * piece, piece)
+        out_ref[:, at] = jnp.dot(left, cols[:, at], preferred_element_type=F32) * scale
+
+    @pl.when(in_mine)
+    def _():
+        at = pl.ds(pl.multiple_of(offset + step * tall, tall), tall)
+        eye = lax.broadcasted_iota(jnp.int32, (tall, tall), 0) == lax.broadcasted_iota(jnp.int32, (tall, tall), 1)
+        out_ref[:, at] = out_ref[:, at] + jnp.where(eye, scalars[1:2, 0:1], 0.0)
+
+
+def on_chip_pairs(scenarios):
+    rows, factors = scenarios.shape
+    scen_size = lax.axis_size("scen")
+    fac_size = lax.axis_size("fac")
+    lines = scen_size // 4
+    half = factors // fac_size
+    width = factors // scen_size
+    vmem = pl.BlockSpec(memory_space=pltpu.VMEM)
+    held = jax.ShapeDtypeStruct((scen_size, 2, rows, half), BF16)
+    dma = pltpu.SemaphoreType.DMA
+    mine, other = pl.pallas_call(
+        functools.partial(gather_kernel, lines),
+        out_shape=(held, held),
+        in_specs=[vmem],
+        out_specs=(vmem, vmem),
+        scratch_shapes=[
+            dma((1,)),
+            dma((2, 1)),
+            dma((3, lines)),
+            dma((2, lines)),
+            dma((2, lines)),
+            dma((2, 2 * lines)),
+            dma((2, scen_size)),
+        ],
+        compiler_params=pltpu.CompilerParams(collective_id=0, has_side_effects=True),
+        name="gather_rows",
+    )(scenarios)
+    mine = mine.reshape(2 * scen_size, rows, half)
+    other = other.reshape(2 * scen_size, rows, half)
+    total_rows = 2 * scen_size * rows
+    tall = 128
+    steps = width // tall
+    shrunk, shrinkage, mean_block = pl.pallas_call(
+        functools.partial(shrink_kernel, steps),
+        grid=(steps,),
+        out_shape=(
+            jax.ShapeDtypeStruct((width, half), F32),
+            jax.ShapeDtypeStruct((1, 1), F32),
+            jax.ShapeDtypeStruct((1, half), F32),
+        ),
+        in_specs=[vmem, vmem],
+        out_specs=(
+            pl.BlockSpec((tall, half), lambda i: (i, 0)),
+            pl.BlockSpec((1, 1), lambda i: (0, 0)),
+            pl.BlockSpec((1, half), lambda i: (0, 0)),
+        ),
+        scratch_shapes=[
+            pltpu.VMEM((total_rows, half), BF16),
+            pltpu.VMEM((total_rows, half), BF16),
+            pltpu.VMEM((width, total_rows), BF16),
+            pltpu.VMEM((8, 128), F32),
+        ],
+        compiler_params=pltpu.CompilerParams(dimension_semantics=("arbitrary",)),
+        name="shrink_rows",
+    )(mine, other)
+    return shrunk, shrinkage.reshape(()), mean_block.reshape(half)
 
 
 def on_device(scenarios):
@@ -53,8 +347,18 @@
 
 
 def solution(mesh):
+    pairs = mesh.shape["fac"] == 2 and mesh.shape["scen"] % 4 == 0
+
+    def step(scenarios):
+        rows, factors = scenarios.shape
+        width = factors // lax.axis_size("scen")
+        gathered = rows * lax.axis_size("scen") * factors * 2 * scenarios.dtype.itemsize
+        if pairs and rows == 8 and width % 128 == 0 and (factors // 2) % 1024 == 0 and gathered <= 2**23:
+            return on_chip_pairs(scenarios)
+        return on_device(scenarios)
+
     return jax.shard_map(
-        on_device,
+        step,
         mesh=mesh,
         in_specs=(P(("scen", "fac"), None),),
         out_specs=(P("scen", "fac"), P(), P("fac")),

time: 181 us -> 42.9 us (0.24)
  blocking collectives: 124 us -> 0 us
  Pallas kernels: 0 us -> 42.1 us
  between operations: 18.5 us -> 0.64 us
  other arithmetic: 12 us -> 0 us
  waiting for transfers between devices: 10.7 us -> 0 us
  matrix products: 6.84 us -> 0 us
  starting transfers between devices: 5.46 us -> 0 us
  local copies, waits for them, and re-layouts: 2 us -> 0 us
    psum x3 -> x0, blocking collectives: 122 us -> none  [the longest x2 80.2 us: on_device(): lax.psum((trace_part, fourth_part), ('scen', 'fac'))]
    pallas_call x0 -> x2, Pallas kernels: none -> 42.1 us  [the longest x1 32.6 us: on_chip_pairs(): pl.pallas_call(functools.partial(gather_kernel, lines), out_shape=(held,...]
    all_gather x1 -> x0, waiting for transfers between devices: 10.7 us -> none  [on_device(): lax.all_gather(wide_cols, 'scen', axis=0, tiled=True)]
    add x3 -> x0, other arithmetic: 8.7 us -> none  [the longest x1 8.69 us: on_device(): shrunk = (1.0 - shrinkage) * covariance + shrinkage * mu_scale * diag_mask]
    dot_general x1 -> x0, matrix products: 6.84 us -> none  [on_device(): lax.dot_general(narrow_all, lax.all_gather(wide_cols, 'scen', axis=0, til...]
    all_to_all x1 -> x0, starting transfers between devices: 5.42 us -> none  [on_device(): lax.all_to_all(local_rows, 'scen', split_axis=1, concat_axis=0, tiled=True)]
    reduce_sum x3 -> x0, other arithmetic: 3.27 us -> none  [the longest x1 1.62 us: on_device(): trace_part = jnp.sum(squared)]
    all_gather x1 -> x0, blocking collectives: 1.98 us -> none  [on_device(): local_rows = lax.all_gather(centered, 'fac', axis=0, tiled=True)]
  transfers between devices with their start and end apart: 2 -> 0, of which waited for: 1 -> 0; matrix products, arithmetic and copies ran while one was open for 1% -> 0% of each run, Pallas kernels for 0% -> 0%
where the time goes in v1:
time: 42.9 us; the launch traced here: 42.8 us
  Pallas kernels  42.1 us (98%)
  between operations  0.64 us (1%)
    pallas_call x1, Pallas kernels, on_chip_pairs(): pl.pallas_call(functools.partial(gather_kernel, lines), out_shape=(held,...  32.6 us
    pallas_call x1, Pallas kernels, on_chip_pairs(): pl.pallas_call(functools.partial(shrink_kernel, steps), grid=(steps,), ou...  9.54 us

profile of v1, /device:TPU:0, one launch (start us, length us, event | category | flops | bytes accessed | tf_op | source)
XLA Modules:
  0.0 42.8 jit_solution(6281560467081179906)
XLA Ops:
  0.6 32.6 %gather_rows.1 = (bf16[16,2,8,4096]{3,2,1,0:T(8,128)(2,1)}, bf16[16,2,8,4096]{3,2,1,0:T(8,128)(2,1)}) custom-call(bf16[8,8192]{1,0:T(8,128)(2,1)} %rows_ref.1), custom_call_target="tpu_custom_call" | custom-call | tf_op jit(solution)/shard_map/gather_rows/pallas_call | solution.py:253
  33.2 9.5 %shrink_rows.1 = (f32[512,4096]{1,0:T(8,128)}, f32[1,1]{1,0:T(1,128)}, f32[1,4096]{1,0:T(1,128)}) custom-call(bf16[32,8,4096]{2,1,0:T(8,128)(2,1)} %bitcast.4, bf16[32,8,4096]{2,1,0:T(8,128)(2,1)} %bitcast.5), custom_call_target="tpu_custom_call" | custom-call | tf_op jit(solution)/shard_map/shrink_rows/pallas_call | solution.py:275

commit v2 on v1

--- a/solution.py
+++ b/solution.py
@@ -248,7 +248,7 @@
     half = factors // fac_size
     width = factors // scen_size
     vmem = pl.BlockSpec(memory_space=pltpu.VMEM)
-    held = jax.ShapeDtypeStruct((scen_size, 2, rows, half), BF16)
+    held = pltpu.VMEM((scen_size, 2, rows, half), BF16)
     dma = pltpu.SemaphoreType.DMA
     mine, other = pl.pallas_call(
         functools.partial(gather_kernel, lines),
@@ -264,7 +264,7 @@
             dma((2, 2 * lines)),
             dma((2, scen_size)),
         ],
-        compiler_params=pltpu.CompilerParams(collective_id=0, has_side_effects=True),
+        compiler_params=pltpu.CompilerParams(collective_id=0, has_side_effects=True, vmem_limit_bytes=2**24),
         name="gather_rows",
     )(scenarios)
     mine = mine.reshape(2 * scen_size, rows, half)
@@ -292,7 +292,7 @@
             pltpu.VMEM((width, total_rows), BF16),
             pltpu.VMEM((8, 128), F32),
         ],
-        compiler_params=pltpu.CompilerParams(dimension_semantics=("arbitrary",)),
+        compiler_params=pltpu.CompilerParams(dimension_semantics=("arbitrary",), vmem_limit_bytes=2**25),
         name="shrink_rows",
     )(mine, other)
     return shrunk, shrinkage.reshape(()), mean_block.reshape(half)

time: 42.9 us -> 38.8 us (0.904)
  Pallas kernels: 42.1 us -> 37.1 us
  local copies, waits for them, and re-layouts: 0 us -> 0.9 us
    pallas_call x1, Pallas kernels: 32.6 us -> 29.8 us  [on_chip_pairs(): pl.pallas_call(functools.partial(gather_kernel, lines), out_shape=(held,...]
    pallas_call x1, Pallas kernels: 9.54 us -> 7.33 us  [on_chip_pairs(): pl.pallas_call(functools.partial(shrink_kernel, steps), grid=(steps,), ou...]
    unnamed x0 -> x2, local copies, waits for them, and re-layouts: none -> 0.9 us
where the time goes in v2:
time: 38.8 us; the launch traced here: 38.6 us
  Pallas kernels  37.1 us (96%)
  local copies, waits for them, and re-layouts  0.9 us (2%)
  between operations  0.65 us (2%)
    pallas_call x1, Pallas kernels, on_chip_pairs(): pl.pallas_call(functools.partial(gather_kernel, lines), out_shape=(held,...  29.8 us
    pallas_call x1, Pallas kernels, on_chip_pairs(): pl.pallas_call(functools.partial(shrink_kernel, steps), grid=(steps,), ou...  7.33 us
    unnamed x2, local copies, waits for them, and re-layouts  0.9 us

profile of v2, /device:TPU:0, one launch (start us, length us, event | category | flops | bytes accessed | tf_op | source)
XLA Modules:
  0.0 38.6 jit_solution(3216955756913986500)
XLA Ops:
  0.6 0.0 copy-start
  0.6 0.9 %copy-done = bf16[8,8192]{1,0:T(8,128)(2,1)S(1)} copy-done((bf16[8,8192]{1,0:T(8,128)(2,1)S(1)}, bf16[8,8192]{1,0:T(8,128)(2,1)}, u32[]{:S(2)}) %copy-start) | copy-done | bytes 131096
  1.5 29.8 %gather_rows.1 = (bf16[16,2,8,4096]{3,2,1,0:T(8,128)(2,1)S(1)}, bf16[16,2,8,4096]{3,2,1,0:T(8,128)(2,1)S(1)}) custom-call(bf16[8,8192]{1,0:T(8,128)(2,1)S(1)} %copy-done), custom_call_target="tpu_custom_call" | custom-call | tf_op jit(solution)/shard_map/gather_rows/pallas_call | solution.py:253
  31.3 7.3 %shrink_rows.1 = (f32[512,4096]{1,0:T(8,128)}, f32[1,1]{1,0:T(1,128)}, f32[1,4096]{1,0:T(1,128)}) custom-call(bf16[32,8,4096]{2,1,0:T(8,128)(2,1)S(1)} %bitcast.4, bf16[32,8,4096]{2,1,0:T(8,128)(2,1)S(1)} %bitcast.5), custom_call_target="tpu_custom_call" | custom-call | tf_op jit(solution)/shard_map/shrink_rows/pallas_call | solution.py:275
Async XLA Ops:
  0.6 0.9 %copy-start = (bf16[8,8192]{1,0:T(8,128)(2,1)S(1)}, bf16[8,8192]{1,0:T(8,128)(2,1)}, u32[]{:S(2)}) copy-start(bf16[8,8192]{1,0:T(8,128)(2,1)} %rows_ref.1) | copy-start | bytes 393220

commit v3 on v2

--- a/solution.py
+++ b/solution.py
@@ -12,7 +12,8 @@
 BF16 = jnp.bfloat16
 
 
-def gather_kernel(lines, rows_ref, mine_ref, other_ref, local_sem, pair_sems, z_sems, x_sems, y_sems, d_sems, core_sems):
+def gather_kernel(lines, rows_ref, mine_ref, other_ref, local_sem, pair_sems, z_sems, x_sems, y_sems, d_sems, line_sems, core_sems):
+    reach = lines // 2
     scen = lax.axis_index("scen")
     fac = lax.axis_index("fac")
     z, y, x = scen // 4, (scen // 2) % 2, scen % 2
@@ -44,121 +45,164 @@
 
     pl.semaphore_wait(barrier, 3 + has_above.astype(jnp.int32) + has_below.astype(jnp.int32))
 
-    def copy(src, dst, sems, i, device):
+    def copy(ref, sems, i, device, sender=0):
         return pltpu.make_async_remote_copy(
-            src_ref=src, dst_ref=dst, send_sem=sems.at[0, i], recv_sem=sems.at[1, i], device_id=device, device_id_type=MESH
+            src_ref=ref,
+            dst_ref=ref,
+            send_sem=sems.at[sender, i],
+            recv_sem=sems.at[1, i],
+            device_id=device,
+            device_id_type=MESH,
         )
 
-    def block(c):
-        return mine_ref.at[c]
-
-    keep = pltpu.make_async_copy(rows_ref.at[:, pl.ds(pl.multiple_of(fac * half, half), half)], mine_ref.at[scen, fac], local_sem.at[0])
+    def core_of(i):
+        return fac if i == 0 else 1 - fac
+
+    def part(k, yy, xx, i):
+        return mine_ref.at[chip(k, yy, xx), core_of(i)]
+
+    def up(k, i):
+        return copy(part(k, y, x, i), z_sems, 2 * k + i, above)
+
+    def down(k, i):
+        return copy(part(k, y, x, i), z_sems, 2 * k + i, below, 2)
+
+    def to_x(k, i):
+        return copy(part(k, y, x, i), x_sems, 2 * k + i, x_next)
+
+    def to_y(k, i):
+        return copy(part(k, y, x, i), y_sems, 2 * k + i, y_next)
+
+    def diag_x(k):
+        return copy(part(k, 1 - y, x, 0), d_sems, 2 * k, x_next)
+
+    def diag_y(k):
+        return copy(part(k, y, 1 - x, 1), d_sems, 2 * k + 1, y_next)
+
+    def diag_up(k, i):
+        return copy(part(k, 1 - y, 1 - x, i), line_sems, 2 * k + i, above)
+
+    def diag_down(k, i):
+        return copy(part(k, 1 - y, 1 - x, i), line_sems, 2 * k + i, below, 2)
+
+    def to_core(c, j):
+        return pltpu.make_async_remote_copy(
+            src_ref=mine_ref.at[c, j],
+            dst_ref=other_ref.at[c, j],
+            send_sem=core_sems.at[0, 2 * c + j],
+            recv_sem=core_sems.at[1, 2 * c + j],
+            device_id=partner,
+            device_id_type=MESH,
+        )
+
+    def start_if(condition, transfer):
+        @pl.when(condition)
+        def _():
+            transfer.start()
+
+    def line_step(k, sign, i):
+        if sign:
+            up(k, i).wait_recv()
+        to_x(k, i).start()
+        to_y(k, i).start()
+        if sign <= 0:
+            start_if(has_above, up(k, i))
+        if sign >= 0:
+            start_if(has_below, down(k, i))
+        to_core(chip(k, y, x), core_of(i)).start()
+
+    def side_step(k, crosses, i):
+        to_x(k, i).wait_recv()
+        if crosses and i == 1:
+            diag_y(k).start()
+        to_core(chip(k, y, 1 - x), core_of(i)).start()
+        to_y(k, i).wait_recv()
+        if crosses and i == 0:
+            diag_x(k).start()
+        to_core(chip(k, 1 - y, x), core_of(i)).start()
+
+    def diag_step(k, sign, d, i):
+        if d == 0 or d > reach:
+            (diag_x, diag_y)[i](k).wait_recv()
+        else:
+            diag_up(k, i).wait_recv()
+        if d < reach:
+            if sign <= 0:
+                start_if(has_above, diag_up(k, i))
+            if sign >= 0:
+                start_if(has_below, diag_down(k, i))
+        to_core(chip(k, 1 - y, 1 - x), core_of(i)).start()
+
+    def each(d, step):
+        for i in range(2):
+            if d == 0:
+                step(z, 0, i)
+                continue
+
+            @pl.when(z - d >= 0)
+            def _():
+                step(z - d, -1, i)
+
+            @pl.when(z + d < lines)
+            def _():
+                step(z + d, 1, i)
+
+    def line(d):
+        each(d, line_step)
+
+    def side(d):
+        each(d, lambda k, sign, i: side_step(k, d == 0 or d > reach, i))
+
+    def diag(d):
+        each(d, lambda k, sign, i: diag_step(k, sign, d, i))
+
+    keep = pltpu.make_async_copy(
+        rows_ref.at[:, pl.ds(pl.multiple_of(fac * half, half), half)], mine_ref.at[scen, fac], local_sem.at[0]
+    )
     keep.start()
-    give = copy(
-        rows_ref.at[:, pl.ds(pl.multiple_of((1 - fac) * half, half), half)], mine_ref.at[scen, fac], pair_sems, 0, partner
+    give = pltpu.make_async_remote_copy(
+        src_ref=rows_ref.at[:, pl.ds(pl.multiple_of((1 - fac) * half, half), half)],
+        dst_ref=mine_ref.at[scen, fac],
+        send_sem=pair_sems.at[0, 0],
+        recv_sem=pair_sems.at[1, 0],
+        device_id=partner,
+        device_id_type=MESH,
     )
     give.start()
     keep.wait()
+    line_step(z, 0, 0)
     give.wait_recv()
-
-    def up(k):
-        return copy(block(chip(k, y, x)), block(chip(k, y, x)), z_sems, k, above)
-
-    def down(k):
-        return pltpu.make_async_remote_copy(
-            src_ref=block(chip(k, y, x)),
-            dst_ref=block(chip(k, y, x)),
-            send_sem=z_sems.at[2, k],
-            recv_sem=z_sems.at[1, k],
-            device_id=below,
-            device_id_type=MESH,
-        )
-
-    def to_x(k):
-        return copy(block(chip(k, y, x)), block(chip(k, y, x)), x_sems, k, x_next)
-
-    def to_y(k):
-        return copy(block(chip(k, y, x)), block(chip(k, y, x)), y_sems, k, y_next)
-
-    def part(c, i):
-        return mine_ref.at[c, :, :, pl.ds(i * mid, mid)]
-
-    def diag_x(k):
-        c = chip(k, 1 - y, x)
-        return copy(part(c, 0), part(c, 0), d_sems, 2 * k, x_next)
-
-    def diag_y(k):
-        c = chip(k, y, 1 - x)
-        return copy(part(c, 1), part(c, 1), d_sems, 2 * k + 1, y_next)
-
-    def to_core(c):
-        return copy(mine_ref.at[c], other_ref.at[c], core_sems, c, partner)
-
-    def line_step(k, ups, downs, arrived):
-        if arrived:
-            up(k).wait_recv()
-        to_x(k).start()
-        to_y(k).start()
-        if ups:
-            @pl.when(has_above)
-            def _():
-                up(k).start()
-        if downs:
-            @pl.when(has_below)
-            def _():
-                down(k).start()
-        to_core(chip(k, y, x)).start()
-
-    def side_step(k):
-        to_x(k).wait_recv()
-        diag_y(k).start()
-        to_core(chip(k, y, 1 - x)).start()
-        to_y(k).wait_recv()
-        diag_x(k).start()
-        to_core(chip(k, 1 - y, x)).start()
-
-    def diag_step(k):
-        diag_x(k).wait_recv()
-        diag_y(k).wait_recv()
-        to_core(chip(k, 1 - y, 1 - x)).start()
-
-    def each(d, step):
-        if d == 0:
-            step(z, 0)
-            return
-
-        @pl.when(z - d >= 0)
+    line_step(z, 0, 1)
+    for d in range(1, lines):
+        line(d)
+        if d >= 2:
+            diag(d - 2)
+        side(d - 1)
+    if lines >= 2:
+        diag(lines - 2)
+    side(lines - 1)
+    diag(lines - 1)
+
+    give.wait_send()
+
+    def sent_if(condition, *transfers):
+        @pl.when(condition)
         def _():
-            step(z - d, -1)
-
-        @pl.when(z + d < lines)
-        def _():
-            step(z + d, 1)
-
-    line_step(z, True, True, False)
-    for d in range(1, lines):
-        each(d, lambda k, sign: line_step(k, sign < 0, sign > 0, True))
-        each(d - 1, lambda k, sign: side_step(k))
-    each(lines - 1, lambda k, sign: side_step(k))
-    for d in range(lines):
-        each(d, lambda k, sign: diag_step(k))
-
-    give.wait_send()
+            for transfer in transfers:
+                transfer.wait_send()
+
     for k in range(lines):
-        to_x(k).wait_send()
-        to_y(k).wait_send()
-        diag_x(k).wait_send()
-        diag_y(k).wait_send()
-
-        @pl.when((k <= z) & has_above)
-        def _():
-            up(k).wait_send()
-
-        @pl.when((k >= z) & has_below)
-        def _():
-            down(k).wait_send()
+        for i in range(2):
+            to_x(k, i).wait_send()
+            to_y(k, i).wait_send()
+            sent_if((k <= z) & has_above, up(k, i))
+            sent_if((k >= z) & has_below, down(k, i))
+            sent_if((k <= z) & (k > z - reach) & has_above, diag_up(k, i))
+            sent_if((k >= z) & (k < z + reach) & has_below, diag_down(k, i))
+        sent_if((k == z) | (k > z + reach) | (k < z - reach), diag_x(k), diag_y(k))
     for c in range(4 * lines):
-        to_core(c).wait()
+        for j in range(2):
+            to_core(c, j).wait()
 
 
 def shrink_kernel(steps, mine_ref, other_ref, out_ref, shrinkage_ref, mean_ref, cols, cols_other, narrow, scalars):
@@ -258,11 +302,12 @@
         scratch_shapes=[
             dma((1,)),
             dma((2, 1)),
-            dma((3, lines)),
-            dma((2, lines)),
-            dma((2, lines)),
+            dma((3, 2 * lines)),
             dma((2, 2 * lines)),
-            dma((2, scen_size)),
+            dma((2, 2 * lines)),
+            dma((2, 2 * lines)),
+            dma((3, 2 * lines)),
+            dma((2, 2 * scen_size)),
         ],
         compiler_params=pltpu.CompilerParams(collective_id=0, has_side_effects=True, vmem_limit_bytes=2**24),
         name="gather_rows",

time: 38.8 us -> 40.9 us (1.054)
  Pallas kernels: 37.1 us -> 39.2 us
    pallas_call x1, Pallas kernels: 29.8 us -> 31.8 us  [on_chip_pairs(): pl.pallas_call(functools.partial(gather_kernel, lines), out_shape=(held,...]
where the time goes in v3:
time: 40.9 us; the launch traced here: 40.7 us
  Pallas kernels  39.2 us (96%)
  local copies, waits for them, and re-layouts  0.9 us (2%)
  between operations  0.65 us (2%)
    pallas_call x1, Pallas kernels, on_chip_pairs(): pl.pallas_call(functools.partial(gather_kernel, lines), out_shape=(held,...  31.8 us
    pallas_call x1, Pallas kernels, on_chip_pairs(): pl.pallas_call(functools.partial(shrink_kernel, steps), grid=(steps,), ou...  7.35 us
    unnamed x2, local copies, waits for them, and re-layouts  0.9 us

profile of v3, /device:TPU:0, one launch (start us, length us, event | category | flops | bytes accessed | tf_op | source)
XLA Modules:
  0.0 40.7 jit_solution(3012658868940906708)
XLA Ops:
  0.6 0.0 copy-start
  0.6 0.9 %copy-done = bf16[8,8192]{1,0:T(8,128)(2,1)S(1)} copy-done((bf16[8,8192]{1,0:T(8,128)(2,1)S(1)}, bf16[8,8192]{1,0:T(8,128)(2,1)}, u32[]{:S(2)}) %copy-start) | copy-done | bytes 131096
  1.5 31.8 %gather_rows.1 = (bf16[16,2,8,4096]{3,2,1,0:T(8,128)(2,1)S(1)}, bf16[16,2,8,4096]{3,2,1,0:T(8,128)(2,1)S(1)}) custom-call(bf16[8,8192]{1,0:T(8,128)(2,1)S(1)} %copy-done), custom_call_target="tpu_custom_call" | custom-call | tf_op jit(solution)/shard_map/gather_rows/pallas_call | solution.py:297
  33.4 7.4 %shrink_rows.1 = (f32[512,4096]{1,0:T(8,128)}, f32[1,1]{1,0:T(1,128)}, f32[1,4096]{1,0:T(1,128)}) custom-call(bf16[32,8,4096]{2,1,0:T(8,128)(2,1)S(1)} %bitcast.4, bf16[32,8,4096]{2,1,0:T(8,128)(2,1)S(1)} %bitcast.5), custom_call_target="tpu_custom_call" | custom-call | tf_op jit(solution)/shard_map/shrink_rows/pallas_call | solution.py:320
Async XLA Ops:
  0.6 0.9 %copy-start = (bf16[8,8192]{1,0:T(8,128)(2,1)S(1)}, bf16[8,8192]{1,0:T(8,128)(2,1)}, u32[]{:S(2)}) copy-start(bf16[8,8192]{1,0:T(8,128)(2,1)} %rows_ref.1) | copy-start | bytes 393220

commit v4 on v3

--- a/solution.py
+++ b/solution.py
@@ -12,8 +12,10 @@
 BF16 = jnp.bfloat16
 
 
-def gather_kernel(lines, rows_ref, mine_ref, other_ref, local_sem, pair_sems, z_sems, x_sems, y_sems, d_sems, line_sems, core_sems):
-    reach = lines // 2
+def gather_kernel(lines, input_ref, mine_ref, other_ref, rows_ref, local_sem, pair_sems, z_sems, x_sems, y_sems, d_sems, line_sems, core_sems):
+    reach = 1
+    load = pltpu.make_async_copy(input_ref, rows_ref, local_sem.at[1])
+    load.start()
     scen = lax.axis_index("scen")
     fac = lax.axis_index("fac")
     z, y, x = scen // 4, (scen // 2) % 2, scen % 2
@@ -156,6 +158,7 @@
     def diag(d):
         each(d, lambda k, sign, i: diag_step(k, sign, d, i))
 
+    load.wait()
     keep = pltpu.make_async_copy(
         rows_ref.at[:, pl.ds(pl.multiple_of(fac * half, half), half)], mine_ref.at[scen, fac], local_sem.at[0]
     )
@@ -297,10 +300,11 @@
     mine, other = pl.pallas_call(
         functools.partial(gather_kernel, lines),
         out_shape=(held, held),
-        in_specs=[vmem],
+        in_specs=[pl.BlockSpec(memory_space=pltpu.HBM)],
         out_specs=(vmem, vmem),
         scratch_shapes=[
-            dma((1,)),
+            pltpu.VMEM((rows, factors), BF16),
+            dma((2,)),
             dma((2, 1)),
             dma((3, 2 * lines)),
             dma((2, 2 * lines)),

time: 40.9 us -> 39.2 us (0.958)
  Pallas kernels: 39.2 us -> 37.5 us
    pallas_call x1, Pallas kernels: 31.8 us -> 30.2 us  [on_chip_pairs(): pl.pallas_call(functools.partial(gather_kernel, lines), out_shape=(held,...]
where the time goes in v4:
time: 39.2 us; the launch traced here: 39 us
  Pallas kernels  37.5 us (96%)
  local copies, waits for them, and re-layouts  0.9 us (2%)
  between operations  0.65 us (2%)
    pallas_call x1, Pallas kernels, on_chip_pairs(): pl.pallas_call(functools.partial(gather_kernel, lines), out_shape=(held,...  30.2 us
    pallas_call x1, Pallas kernels, on_chip_pairs(): pl.pallas_call(functools.partial(shrink_kernel, steps), grid=(steps,), ou...  7.33 us
    unnamed x2, local copies, waits for them, and re-layouts  0.9 us

profile of v4, /device:TPU:0, one launch (start us, length us, event | category | flops | bytes accessed | tf_op | source)
XLA Modules:
  0.0 39.0 jit_solution(17021225373706097220)
XLA Ops:
  0.6 0.0 copy-start
  0.6 0.9 %copy-done = bf16[8,8192]{1,0:T(8,128)(2,1)S(1)} copy-done((bf16[8,8192]{1,0:T(8,128)(2,1)S(1)}, bf16[8,8192]{1,0:T(8,128)(2,1)}, u32[]{:S(2)}) %copy-start) | copy-done | bytes 131096
  1.5 30.2 %gather_rows.1 = (bf16[16,2,8,4096]{3,2,1,0:T(8,128)(2,1)S(1)}, bf16[16,2,8,4096]{3,2,1,0:T(8,128)(2,1)S(1)}) custom-call(bf16[8,8192]{1,0:T(8,128)(2,1)S(1)} %copy-done), custom_call_target="tpu_custom_call" | custom-call | tf_op jit(solution)/shard_map/gather_rows/pallas_call | solution.py:300
  31.7 7.3 %shrink_rows.1 = (f32[512,4096]{1,0:T(8,128)}, f32[1,1]{1,0:T(1,128)}, f32[1,4096]{1,0:T(1,128)}) custom-call(bf16[32,8,4096]{2,1,0:T(8,128)(2,1)S(1)} %bitcast.4, bf16[32,8,4096]{2,1,0:T(8,128)(2,1)S(1)} %bitcast.5), custom_call_target="tpu_custom_call" | custom-call | tf_op jit(solution)/shard_map/shrink_rows/pallas_call | solution.py:324
Async XLA Ops:
  0.6 0.9 %copy-start = (bf16[8,8192]{1,0:T(8,128)(2,1)S(1)}, bf16[8,8192]{1,0:T(8,128)(2,1)}, u32[]{:S(2)}) copy-start(bf16[8,8192]{1,0:T(8,128)(2,1)} %input_ref.1) | copy-start | bytes 393220
